TPU v7x, 32 devices: a whole 2x2x4 slice. The times are simulated.
32 devices in a mesh: blk: 16 (over z, y, x), rep: 2 (over core).
Axes of the slice: x: 2, y: 2, z: 4, core: 2. Of those that a mesh axis runs over, the one named last changes fastest.
Arguments:
- points: float32 [16, 3, 8192], P('blk'), may hold values from -6 to 6
- normals: float32 [16, 3, 8192], P('blk'), may hold values from -6 to 6
- src_block: int32 [8, 16, 1, 16], P(None, 'blk', None, 'rep'), may hold values from 0 to 63
- tgt_index: int32 [8, 16, 1, 16, 128], P(None, 'blk', None, 'rep'), may hold values from 0 to 8191
- active: int32 [8, 16, 1], P(None, 'blk'), may hold values from 0 to 16
Outputs:
- diag_hess: float32 [16, 36], P('blk')
- gradient: float32 [16, 6], P('blk')
- pair_hess: float32 [8, 16, 1, 36], P(None, 'blk')
Inputs may be any that keep to these rules, and one draw needn't show every extreme that they name: Slots j with j >= active contribute nothing.
All inputs are finite; a program needn't handle non-finite values.
Results may differ from a plain program's by a relative error of at most 0.00017.
Values sent between devices are 32-bit elements; how exact they have to be, the bound alone decides.
A program may use at most 64 MiB of HBM per device.

v0:
```python
import jax
import jax.numpy as jnp
from jax import lax
from jax.sharding import PartitionSpec as P

NB = 16
BLOCK = 128


def passed_along(block, axis, distance):
    devices = range(lax.axis_size(axis))
    route = [((i - distance) % len(devices), i) for i in devices]
    return lax.ppermute(block, axis, route)


def body(points, normals, src_block, tgt_index, active):
    count = points.shape[0]
    npts = points.shape[2]
    rounds = src_block.shape[0]
    per_rep = src_block.shape[3]
    slots = per_rep * BLOCK
    half_id = lax.axis_index("rep")
    lane_block = jnp.arange(slots, dtype=jnp.int32) // BLOCK + half_id * per_rep
    lanes = jnp.arange(BLOCK, dtype=jnp.int32)
    source_ids = jnp.arange(count, dtype=jnp.int32)
    target_ids = jnp.arange(count, dtype=jnp.int32)
    flat_src = jnp.moveaxis(points, 1, 0).reshape(3, count * npts)
    tile = jnp.concatenate([points, normals], axis=1)

    def round_terms(k, arrived):
        blocks = lax.dynamic_index_in_dim(src_block, k, 0, keepdims=False)
        targets = lax.dynamic_index_in_dim(tgt_index, k, 0, keepdims=False).reshape(
            count, count, slots
        )
        sidx = (
            source_ids[:, None, None, None] * npts + blocks[:, :, :, None] * BLOCK + lanes
        ).reshape(count, count, slots)
        tidx = target_ids[None, :, None] * npts + targets
        p = flat_src[:, sidx]
        flat_tgt = jnp.moveaxis(arrived, 1, 0).reshape(6, count * npts)
        picked = flat_tgt[:, tidx]
        q = picked[:3]
        n = picked[3:]
        limit = lax.dynamic_index_in_dim(active, k, 0, keepdims=False)
        live = (lane_block[None, None, :] < limit[:, :, None]).astype(jnp.float32)
        resid = jnp.sum(n * (p - q), axis=0)
        weight = live / (1.0 + resid * resid)
        jacob = jnp.stack(
            [
                p[1] * n[2] - p[2] * n[1],
                p[2] * n[0] - p[0] * n[2],
                p[0] * n[1] - p[1] * n[0],
                n[0],
                n[1],
                n[2],
            ]
        )
        gram = jnp.einsum(
            "istl,jstl->stij", jacob * weight, jacob, precision=lax.Precision.HIGHEST
        ) / (NB * BLOCK)
        push = jnp.einsum(
            "istl,stl->sti", jacob, weight * resid, precision=lax.Precision.HIGHEST
        ) / (NB * BLOCK)
        return (gram.reshape(count, count, 36), push)

    def advance(current):
        joined = passed_along(current, "blk", 1)
        return joined

    store = jnp.zeros((count, 42), jnp.float32)

    def one_round(k, carry):
        current, pair_out, own_h, own_g, kept = carry
        current = advance(current)
        gram, push = round_terms(k, current)
        pair_out = lax.dynamic_update_index_in_dim(pair_out, gram, k, 0)
        own_h = own_h + gram.sum(1)
        own_g = own_g + push.sum(1)
        remote = jnp.concatenate([gram.sum(0), -push.sum(0)], axis=1)
        kept = passed_along(kept, "blk", 1) + remote
        return (current, pair_out, own_h, own_g, kept)

    start_carry = (
        tile,
        jnp.zeros((rounds, count, count, 36), jnp.float32),
        jnp.zeros((count, 36), jnp.float32),
        jnp.zeros((count, 6), jnp.float32),
        store,
    )
    final = lax.fori_loop(0, rounds, one_round, start_carry)
    pair_out, own_h, own_g, kept = (final[1], final[2], final[3], final[4])
    coming = passed_along(kept, "blk", -rounds)
    own_all = jnp.concatenate([own_h, own_g], axis=1) + coming
    total, pair_total = lax.psum((own_all, pair_out), "rep")
    scale = 2.0 * rounds * count
    return (total[:, :36] / scale, total[:, 36:] / scale, pair_total)


def solution(mesh):
    return jax.shard_map(
        body,
        mesh=mesh,
        in_specs=(
            P("blk", None, None),
            P("blk", None, None),
            P(None, "blk", None, "rep"),
            P(None, "blk", None, "rep", None),
            P(None, "blk", None),
        ),
        out_specs=(P("blk", None), P("blk", None), P(None, "blk", None, None)),
        check_vma=False,
    )
```

profile of v0, /device:TPU:0, one launch (start us, length us, event | category | flops | bytes accessed | tf_op | source)
XLA Modules:
  0.0 184.7 jit_solution(1164484923509622730)
XLA Ops:
  0.7 3.4 %copy.18 = f32[1,3,8192]{1,2,0:T(8,128)} copy(f32[1,3,8192]{2,0,1:T(1,128)} %param.7) | data formatting | bytes 196608 | tf_op args[0]
  4.3 171.7 %while.22 = (s32[]{:T(128)}, f32[1,6,8192]{2,0,1:T(1,128)S(1)}, f32[8,1,1,36]{3,2,1,0:T(1,128)S(1)}, f32[1,36]{1,0:T(1,128)S(1)}, f32[1,6]{1,0:T(1,128)S(1)}, /*...) while((s32[]{:T(128)}, f32[1,6,8192]{2,0,1:T(1,128)S(1)}, ...), condition=%wide.region_2.3_spmd.clone, body=%wide.region_0.2_spmd.clone.sunk | while | flops 601357 | bytes 2068545 | solution.py:90
  4.3 3.0 %collective-permute-start = (f32[1,6,8192]{2,0,1:T(1,128)S(1)}, f32[1,6,8192]{2,0,1:T(1,128)S(1)}, u32[]{:S(2)}, u32[]{:S(2)}) collective-permute-start(f32[1,6,8192]{2,0,1:T(1,128)S(1)} %get-tuple-element.382), channel_id=1, source_target_pairs={{30,0},{0,2},{2,4},{4,6},{6,8},{8,10},{10,12},{12,14},{14,16},{16,... | collective-permute-start | bytes 589832 | tf_op jit(solution)/shard_map/while/body/eval_jaxpr/ppermute | solution.py:13
  7.4 1.5 collective-permute-start.1
  10.9 5.0 %gather_fusion.1 = f32[1024,3]{1,0:T(8,128)S(1)} fusion(f32[3,8192]{0,1:T(8,128)} %get-tuple-element.401, s32[1024]{0:T(1024)S(1)} %broadcast_clamp_fusion.5), kind=kCustom, calls=%fused_computation.clone.clone.1 | custom fusion | bytes 28672 | tf_op jit(solution)/shard_map/while/body/eval_jaxpr/gather | solution.py:39
  16.3 2.7 %copy.44 = f32[1,6,8192]{1,2,0:T(8,128)} copy(f32[1,6,8192]{2,0,1:T(1,128)S(1)} %collective-permute-done) | data formatting | bytes 393216 | tf_op jit(solution)/shard_map/while/body/eval_jaxpr/ppermute | solution.py:13
  19.0 5.0 %gather_fusion = f32[1024,6]{1,0:T(8,128)S(1)} fusion(f32[6,8192]{0,1:T(8,128)} %bitcast.109, s32[1024]{0:T(1024)S(1)} %broadcast_clamp_fusion.4), kind=kCustom, calls=%fused_computation.1.clone.clone.1 | custom fusion | bytes 53248 | tf_op jit(solution)/shard_map/while/body/eval_jaxpr/gather | solution.py:41
  24.5 1.2 subtract_reduce_fusion.4
  28.7 1.5 collective-permute-start.1
  32.3 5.0 %gather_fusion.1 = f32[1024,3]{1,0:T(8,128)S(1)} fusion(f32[3,8192]{0,1:T(8,128)} %get-tuple-element.401, s32[1024]{0:T(1024)S(1)} %broadcast_clamp_fusion.5), kind=kCustom, calls=%fused_computation.clone.clone.1 | custom fusion | bytes 28672 | tf_op jit(solution)/shard_map/while/body/eval_jaxpr/gather | solution.py:39
  37.3 2.7 %copy.44 = f32[1,6,8192]{1,2,0:T(8,128)} copy(f32[1,6,8192]{2,0,1:T(1,128)S(1)} %collective-permute-done) | data formatting | bytes 393216 | tf_op jit(solution)/shard_map/while/body/eval_jaxpr/ppermute | solution.py:13
  40.0 5.0 %gather_fusion = f32[1024,6]{1,0:T(8,128)S(1)} fusion(f32[6,8192]{0,1:T(8,128)} %bitcast.109, s32[1024]{0:T(1024)S(1)} %broadcast_clamp_fusion.4), kind=kCustom, calls=%fused_computation.1.clone.clone.1 | custom fusion | bytes 53248 | tf_op jit(solution)/shard_map/while/body/eval_jaxpr/gather | solution.py:41
  45.6 1.2 subtract_reduce_fusion.4
  48.6 1.5 collective-permute-start
  50.1 1.5 collective-permute-start.1
  53.6 5.0 %gather_fusion.1 = f32[1024,3]{1,0:T(8,128)S(1)} fusion(f32[3,8192]{0,1:T(8,128)} %get-tuple-element.401, s32[1024]{0:T(1024)S(1)} %broadcast_clamp_fusion.5), kind=kCustom, calls=%fused_computation.clone.clone.1 | custom fusion | bytes 28672 | tf_op jit(solution)/shard_map/while/body/eval_jaxpr/gather | solution.py:39
  58.7 2.7 %copy.44 = f32[1,6,8192]{1,2,0:T(8,128)} copy(f32[1,6,8192]{2,0,1:T(1,128)S(1)} %collective-permute-done) | data formatting | bytes 393216 | tf_op jit(solution)/shard_map/while/body/eval_jaxpr/ppermute | solution.py:13
  61.4 5.0 %gather_fusion = f32[1024,6]{1,0:T(8,128)S(1)} fusion(f32[6,8192]{0,1:T(8,128)} %bitcast.109, s32[1024]{0:T(1024)S(1)} %broadcast_clamp_fusion.4), kind=kCustom, calls=%fused_computation.1.clone.clone.1 | custom fusion | bytes 53248 | tf_op jit(solution)/shard_map/while/body/eval_jaxpr/gather | solution.py:41
  66.9 1.2 subtract_reduce_fusion.4
  70.0 1.5 collective-permute-start
  71.5 1.5 collective-permute-start.1
  75.0 5.0 %gather_fusion.1 = f32[1024,3]{1,0:T(8,128)S(1)} fusion(f32[3,8192]{0,1:T(8,128)} %get-tuple-element.401, s32[1024]{0:T(1024)S(1)} %broadcast_clamp_fusion.5), kind=kCustom, calls=%fused_computation.clone.clone.1 | custom fusion | bytes 28672 | tf_op jit(solution)/shard_map/while/body/eval_jaxpr/gather | solution.py:39
  80.0 2.7 %copy.44 = f32[1,6,8192]{1,2,0:T(8,128)} copy(f32[1,6,8192]{2,0,1:T(1,128)S(1)} %collective-permute-done) | data formatting | bytes 393216 | tf_op jit(solution)/shard_map/while/body/eval_jaxpr/ppermute | solution.py:13
  82.7 5.0 %gather_fusion = f32[1024,6]{1,0:T(8,128)S(1)} fusion(f32[6,8192]{0,1:T(8,128)} %bitcast.109, s32[1024]{0:T(1024)S(1)} %broadcast_clamp_fusion.4), kind=kCustom, calls=%fused_computation.1.clone.clone.1 | custom fusion | bytes 53248 | tf_op jit(solution)/shard_map/while/body/eval_jaxpr/gather | solution.py:41
  91.3 1.5 collective-permute-start
  92.8 1.5 collective-permute-start.1
  96.4 5.0 %gather_fusion.1 = f32[1024,3]{1,0:T(8,128)S(1)} fusion(f32[3,8192]{0,1:T(8,128)} %get-tuple-element.401, s32[1024]{0:T(1024)S(1)} %broadcast_clamp_fusion.5), kind=kCustom, calls=%fused_computation.clone.clone.1 | custom fusion | bytes 28672 | tf_op jit(solution)/shard_map/while/body/eval_jaxpr/gather | solution.py:39
  101.4 2.7 %copy.44 = f32[1,6,8192]{1,2,0:T(8,128)} copy(f32[1,6,8192]{2,0,1:T(1,128)S(1)} %collective-permute-done) | data formatting | bytes 393216 | tf_op jit(solution)/shard_map/while/body/eval_jaxpr/ppermute | solution.py:13
  104.1 5.0 %gather_fusion = f32[1024,6]{1,0:T(8,128)S(1)} fusion(f32[6,8192]{0,1:T(8,128)} %bitcast.109, s32[1024]{0:T(1024)S(1)} %broadcast_clamp_fusion.4), kind=kCustom, calls=%fused_computation.1.clone.clone.1 | custom fusion | bytes 53248 | tf_op jit(solution)/shard_map/while/body/eval_jaxpr/gather | solution.py:41
  109.7 1.2 subtract_reduce_fusion.4
  112.7 1.5 collective-permute-start
  114.2 1.5 collective-permute-start.1
  117.7 5.0 %gather_fusion.1 = f32[1024,3]{1,0:T(8,128)S(1)} fusion(f32[3,8192]{0,1:T(8,128)} %get-tuple-element.401, s32[1024]{0:T(1024)S(1)} %broadcast_clamp_fusion.5), kind=kCustom, calls=%fused_computation.clone.clone.1 | custom fusion | bytes 28672 | tf_op jit(solution)/shard_map/while/body/eval_jaxpr/gather | solution.py:39
  122.8 2.7 %copy.44 = f32[1,6,8192]{1,2,0:T(8,128)} copy(f32[1,6,8192]{2,0,1:T(1,128)S(1)} %collective-permute-done) | data formatting | bytes 393216 | tf_op jit(solution)/shard_map/while/body/eval_jaxpr/ppermute | solution.py:13
  125.5 5.0 %gather_fusion = f32[1024,6]{1,0:T(8,128)S(1)} fusion(f32[6,8192]{0,1:T(8,128)} %bitcast.109, s32[1024]{0:T(1024)S(1)} %broadcast_clamp_fusion.4), kind=kCustom, calls=%fused_computation.1.clone.clone.1 | custom fusion | bytes 53248 | tf_op jit(solution)/shard_map/while/body/eval_jaxpr/gather | solution.py:41
  134.1 1.5 collective-permute-start
  135.6 1.5 collective-permute-start.1
  139.1 5.0 %gather_fusion.1 = f32[1024,3]{1,0:T(8,128)S(1)} fusion(f32[3,8192]{0,1:T(8,128)} %get-tuple-element.401, s32[1024]{0:T(1024)S(1)} %broadcast_clamp_fusion.5), kind=kCustom, calls=%fused_computation.clone.clone.1 | custom fusion | bytes 28672 | tf_op jit(solution)/shard_map/while/body/eval_jaxpr/gather | solution.py:39
  144.1 2.7 %copy.44 = f32[1,6,8192]{1,2,0:T(8,128)} copy(f32[1,6,8192]{2,0,1:T(1,128)S(1)} %collective-permute-done) | data formatting | bytes 393216 | tf_op jit(solution)/shard_map/while/body/eval_jaxpr/ppermute | solution.py:13
  146.8 5.0 %gather_fusion = f32[1024,6]{1,0:T(8,128)S(1)} fusion(f32[6,8192]{0,1:T(8,128)} %bitcast.109, s32[1024]{0:T(1024)S(1)} %broadcast_clamp_fusion.4), kind=kCustom, calls=%fused_computation.1.clone.clone.1 | custom fusion | bytes 53248 | tf_op jit(solution)/shard_map/while/body/eval_jaxpr/gather | solution.py:41
  152.4 1.2 subtract_reduce_fusion.4
  155.4 1.5 collective-permute-start
  159.1 5.0 %gather_fusion.1 = f32[1024,3]{1,0:T(8,128)S(1)} fusion(f32[3,8192]{0,1:T(8,128)} %get-tuple-element.401, s32[1024]{0:T(1024)S(1)} %broadcast_clamp_fusion.5), kind=kCustom, calls=%fused_computation.clone.clone.1 | custom fusion | bytes 28672 | tf_op jit(solution)/shard_map/while/body/eval_jaxpr/gather | solution.py:39
  164.7 2.7 %copy.44 = f32[1,6,8192]{1,2,0:T(8,128)} copy(f32[1,6,8192]{2,0,1:T(1,128)S(1)} %collective-permute-done) | data formatting | bytes 393216 | tf_op jit(solution)/shard_map/while/body/eval_jaxpr/ppermute | solution.py:13
  167.4 5.0 %gather_fusion = f32[1024,6]{1,0:T(8,128)S(1)} fusion(f32[6,8192]{0,1:T(8,128)} %bitcast.109, s32[1024]{0:T(1024)S(1)} %broadcast_clamp_fusion.4), kind=kCustom, calls=%fused_computation.1.clone.clone.1 | custom fusion | bytes 53248 | tf_op jit(solution)/shard_map/while/body/eval_jaxpr/gather | solution.py:41
  176.0 2.0 %collective-permute-start.2 = (f32[1,42]{1,0:T(1,128)S(1)}, f32[1,42]{1,0:T(1,128)S(1)}, u32[]{:S(2)}, u32[]{:S(2)}) collective-permute-start(f32[1,42]{1,0:T(1,128)S(1)} %get-tuple-element.207), channel_id=1, source_target_pairs={{16,0},{18,2},{20,4},{22,6},{24,8},{26,10},{28,12},{30,14},{0,16},... | collective-permute-start | bytes 512 | tf_op jit(solution)/shard_map/ppermute | solution.py:13
  178.1 2.4 %collective-permute-done.2 = f32[1,42]{1,0:T(1,128)S(1)} collective-permute-done((f32[1,42]{1,0:T(1,128)S(1)}, f32[1,42]{1,0:T(1,128)S(1)}, u32[]{:S(2)}, u32[]{:S(2)}) %collective-permute-start.2) | collective-permute-done | bytes 200 | tf_op jit(solution)/shard_map/ppermute | solution.py:13
  180.6 3.0 %all-reduce = (f32[1,42]{1,0:T(1,128)S(1)}, f32[8,1,1,36]{3,2,1,0:T(1,128)}) all-reduce(f32[1,42]{1,0:T(1,128)S(1)} %maximum_add_fusion.1, f32[8,1,1,36]{3,2,1,0:T(1,128)S(1)} %get-tuple-element.208), channel_id=1, replica_groups=mesh['blk'=16,'rep'=2] {'rep'}, use_global_device_ids=true, to_apply=%region_3.4 | all-reduce | flops 330 | bytes 2640 | tf_op jit(solution)/shard_map/psum | solution.py:94
  (243 shorter events, 42.2 us)
Async XLA Ops:
  0.6 3.5 %copy-start = (f32[1,3,8192]{2,0,1:T(1,128)S(1)}, f32[1,3,8192]{2,0,1:T(1,128)}, u32[]{:S(2)}) copy-start(f32[1,3,8192]{2,0,1:T(1,128)} %param.7) | copy-start | bytes 294916
  0.6 3.5 %copy-start.1 = (f32[1,3,8192]{2,0,1:T(1,128)S(1)}, f32[1,3,8192]{2,0,1:T(1,128)}, u32[]{:S(2)}) copy-start(f32[1,3,8192]{2,0,1:T(1,128)} %param.8) | copy-start | bytes 294916
  0.7 3.7 %copy-start.2 = (s32[8,1,1]{0,2,1:T(1,128)S(1)}, s32[8,1,1]{0,2,1:T(1,128)}, u32[]{:S(2)}) copy-start(s32[8,1,1]{0,2,1:T(1,128)} %param.11) | copy-start | bytes 100
  4.3 11.9 %collective-permute-start = (f32[1,6,8192]{2,0,1:T(1,128)S(1)}, f32[1,6,8192]{2,0,1:T(1,128)S(1)}, u32[]{:S(2)}, u32[]{:S(2)}) collective-permute-start(f32[1,6,8192]{2,0,1:T(1,128)S(1)} %get-tuple-element.382), channel_id=1, source_target_pairs={{30,0},{0,2},{2,4},{4,6},{6,8},{8,10},{10,12},{12,14},{14,16},{16,... | collective-permute-start | bytes 589832 | tf_op jit(solution)/shard_map/while/body/eval_jaxpr/ppermute | solution.py:13
  7.4 20.1 %collective-permute-start.1 = (f32[1,42]{1,0:T(1,128)S(1)}, f32[1,42]{1,0:T(1,128)S(1)}, u32[]{:S(2)}, u32[]{:S(2)}) collective-permute-start(f32[1,42]{1,0:T(1,128)S(1)} %broadcast_select_fusion.4), channel_id=1, source_target_pairs={{30,0},{0,2},{2,4},{4,6},{6,8},{8,10},{10,12},{12,14},{14,16},{16,... | collective-permute-start | bytes 512 | tf_op jit(solution)/shard_map/while/body/eval_jaxpr/ppermute | solution.py:13
  27.6 9.7 %collective-permute-start = (f32[1,6,8192]{2,0,1:T(1,128)S(1)}, f32[1,6,8192]{2,0,1:T(1,128)S(1)}, u32[]{:S(2)}, u32[]{:S(2)}) collective-permute-start(f32[1,6,8192]{2,0,1:T(1,128)S(1)} %get-tuple-element.382), channel_id=1, source_target_pairs={{30,0},{0,2},{2,4},{4,6},{6,8},{8,10},{10,12},{12,14},{14,16},{16,... | collective-permute-start | bytes 589832 | tf_op jit(solution)/shard_map/while/body/eval_jaxpr/ppermute | solution.py:13
  28.7 19.8 %collective-permute-start.1 = (f32[1,42]{1,0:T(1,128)S(1)}, f32[1,42]{1,0:T(1,128)S(1)}, u32[]{:S(2)}, u32[]{:S(2)}) collective-permute-start(f32[1,42]{1,0:T(1,128)S(1)} %broadcast_select_fusion.4), channel_id=1, source_target_pairs={{30,0},{0,2},{2,4},{4,6},{6,8},{8,10},{10,12},{12,14},{14,16},{16,... | collective-permute-start | bytes 512 | tf_op jit(solution)/shard_map/while/body/eval_jaxpr/ppermute | solution.py:13
  48.6 10.0 %collective-permute-start = (f32[1,6,8192]{2,0,1:T(1,128)S(1)}, f32[1,6,8192]{2,0,1:T(1,128)S(1)}, u32[]{:S(2)}, u32[]{:S(2)}) collective-permute-start(f32[1,6,8192]{2,0,1:T(1,128)S(1)} %get-tuple-element.382), channel_id=1, source_target_pairs={{30,0},{0,2},{2,4},{4,6},{6,8},{8,10},{10,12},{12,14},{14,16},{16,... | collective-permute-start | bytes 589832 | tf_op jit(solution)/shard_map/while/body/eval_jaxpr/ppermute | solution.py:13
  50.1 19.8 %collective-permute-start.1 = (f32[1,42]{1,0:T(1,128)S(1)}, f32[1,42]{1,0:T(1,128)S(1)}, u32[]{:S(2)}, u32[]{:S(2)}) collective-permute-start(f32[1,42]{1,0:T(1,128)S(1)} %broadcast_select_fusion.4), channel_id=1, source_target_pairs={{30,0},{0,2},{2,4},{4,6},{6,8},{8,10},{10,12},{12,14},{14,16},{16,... | collective-permute-start | bytes 512 | tf_op jit(solution)/shard_map/while/body/eval_jaxpr/ppermute | solution.py:13
  70.0 10.0 %collective-permute-start = (f32[1,6,8192]{2,0,1:T(1,128)S(1)}, f32[1,6,8192]{2,0,1:T(1,128)S(1)}, u32[]{:S(2)}, u32[]{:S(2)}) collective-permute-start(f32[1,6,8192]{2,0,1:T(1,128)S(1)} %get-tuple-element.382), channel_id=1, source_target_pairs={{30,0},{0,2},{2,4},{4,6},{6,8},{8,10},{10,12},{12,14},{14,16},{16,... | collective-permute-start | bytes 589832 | tf_op jit(solution)/shard_map/while/body/eval_jaxpr/ppermute | solution.py:13
  71.5 19.8 %collective-permute-start.1 = (f32[1,42]{1,0:T(1,128)S(1)}, f32[1,42]{1,0:T(1,128)S(1)}, u32[]{:S(2)}, u32[]{:S(2)}) collective-permute-start(f32[1,42]{1,0:T(1,128)S(1)} %broadcast_select_fusion.4), channel_id=1, source_target_pairs={{30,0},{0,2},{2,4},{4,6},{6,8},{8,10},{10,12},{12,14},{14,16},{16,... | collective-permute-start | bytes 512 | tf_op jit(solution)/shard_map/while/body/eval_jaxpr/ppermute | solution.py:13
  91.3 10.0 %collective-permute-start = (f32[1,6,8192]{2,0,1:T(1,128)S(1)}, f32[1,6,8192]{2,0,1:T(1,128)S(1)}, u32[]{:S(2)}, u32[]{:S(2)}) collective-permute-start(f32[1,6,8192]{2,0,1:T(1,128)S(1)} %get-tuple-element.382), channel_id=1, source_target_pairs={{30,0},{0,2},{2,4},{4,6},{6,8},{8,10},{10,12},{12,14},{14,16},{16,... | collective-permute-start | bytes 589832 | tf_op jit(solution)/shard_map/while/body/eval_jaxpr/ppermute | solution.py:13
  92.8 19.8 %collective-permute-start.1 = (f32[1,42]{1,0:T(1,128)S(1)}, f32[1,42]{1,0:T(1,128)S(1)}, u32[]{:S(2)}, u32[]{:S(2)}) collective-permute-start(f32[1,42]{1,0:T(1,128)S(1)} %broadcast_select_fusion.4), channel_id=1, source_target_pairs={{30,0},{0,2},{2,4},{4,6},{6,8},{8,10},{10,12},{12,14},{14,16},{16,... | collective-permute-start | bytes 512 | tf_op jit(solution)/shard_map/while/body/eval_jaxpr/ppermute | solution.py:13
  112.7 10.0 %collective-permute-start = (f32[1,6,8192]{2,0,1:T(1,128)S(1)}, f32[1,6,8192]{2,0,1:T(1,128)S(1)}, u32[]{:S(2)}, u32[]{:S(2)}) collective-permute-start(f32[1,6,8192]{2,0,1:T(1,128)S(1)} %get-tuple-element.382), channel_id=1, source_target_pairs={{30,0},{0,2},{2,4},{4,6},{6,8},{8,10},{10,12},{12,14},{14,16},{16,... | collective-permute-start | bytes 589832 | tf_op jit(solution)/shard_map/while/body/eval_jaxpr/ppermute | solution.py:13
  114.2 19.8 %collective-permute-start.1 = (f32[1,42]{1,0:T(1,128)S(1)}, f32[1,42]{1,0:T(1,128)S(1)}, u32[]{:S(2)}, u32[]{:S(2)}) collective-permute-start(f32[1,42]{1,0:T(1,128)S(1)} %broadcast_select_fusion.4), channel_id=1, source_target_pairs={{30,0},{0,2},{2,4},{4,6},{6,8},{8,10},{10,12},{12,14},{14,16},{16,... | collective-permute-start | bytes 512 | tf_op jit(solution)/shard_map/while/body/eval_jaxpr/ppermute | solution.py:13
  134.1 10.0 %collective-permute-start = (f32[1,6,8192]{2,0,1:T(1,128)S(1)}, f32[1,6,8192]{2,0,1:T(1,128)S(1)}, u32[]{:S(2)}, u32[]{:S(2)}) collective-permute-start(f32[1,6,8192]{2,0,1:T(1,128)S(1)} %get-tuple-element.382), channel_id=1, source_target_pairs={{30,0},{0,2},{2,4},{4,6},{6,8},{8,10},{10,12},{12,14},{14,16},{16,... | collective-permute-start | bytes 589832 | tf_op jit(solution)/shard_map/while/body/eval_jaxpr/ppermute | solution.py:13
  135.6 19.8 %collective-permute-start.1 = (f32[1,42]{1,0:T(1,128)S(1)}, f32[1,42]{1,0:T(1,128)S(1)}, u32[]{:S(2)}, u32[]{:S(2)}) collective-permute-start(f32[1,42]{1,0:T(1,128)S(1)} %broadcast_select_fusion.4), channel_id=1, source_target_pairs={{30,0},{0,2},{2,4},{4,6},{6,8},{8,10},{10,12},{12,14},{14,16},{16,... | collective-permute-start | bytes 512 | tf_op jit(solution)/shard_map/while/body/eval_jaxpr/ppermute | solution.py:13
  155.4 9.3 %collective-permute-start = (f32[1,6,8192]{2,0,1:T(1,128)S(1)}, f32[1,6,8192]{2,0,1:T(1,128)S(1)}, u32[]{:S(2)}, u32[]{:S(2)}) collective-permute-start(f32[1,6,8192]{2,0,1:T(1,128)S(1)} %get-tuple-element.382), channel_id=1, source_target_pairs={{30,0},{0,2},{2,4},{4,6},{6,8},{8,10},{10,12},{12,14},{14,16},{16,... | collective-permute-start | bytes 589832 | tf_op jit(solution)/shard_map/while/body/eval_jaxpr/ppermute | solution.py:13
  156.9 19.0 %collective-permute-start.1 = (f32[1,42]{1,0:T(1,128)S(1)}, f32[1,42]{1,0:T(1,128)S(1)}, u32[]{:S(2)}, u32[]{:S(2)}) collective-permute-start(f32[1,42]{1,0:T(1,128)S(1)} %broadcast_select_fusion.4), channel_id=1, source_target_pairs={{30,0},{0,2},{2,4},{4,6},{6,8},{8,10},{10,12},{12,14},{14,16},{16,... | collective-permute-start | bytes 512 | tf_op jit(solution)/shard_map/while/body/eval_jaxpr/ppermute | solution.py:13
  176.0 4.5 %collective-permute-start.2 = (f32[1,42]{1,0:T(1,128)S(1)}, f32[1,42]{1,0:T(1,128)S(1)}, u32[]{:S(2)}, u32[]{:S(2)}) collective-permute-start(f32[1,42]{1,0:T(1,128)S(1)} %get-tuple-element.207), channel_id=1, source_target_pairs={{16,0},{18,2},{20,4},{22,6},{24,8},{26,10},{28,12},{30,14},{0,16},... | collective-permute-start | bytes 512 | tf_op jit(solution)/shard_map/ppermute | solution.py:13
where the time goes:
time: 186 us; the launch traced here: 185 us
  local copies, waits for them, and re-layouts  122 us (66%)
  other arithmetic  26.3 us (14%)
  starting transfers between devices  25.7 us (14%)
  waiting for transfers between devices  3.48 us (2%)
  blocking collectives  3.04 us (2%)
  matrix products  2.67 us (1%)
    gather x8, local copies, waits for them, and re-layouts, round_terms(): picked = flat_tgt[:, tidx]  39.9 us
    gather x8, local copies, waits for them, and re-layouts, round_terms(): p = flat_src[:, sidx]  39.9 us
    ppermute x17, starting transfers between devices, passed_along(): return lax.ppermute(block, axis, route)  25.7 us
    ppermute x8, local copies, waits for them, and re-layouts, passed_along(): return lax.ppermute(block, axis, route)  21.6 us
    sub x8, other arithmetic, round_terms(): p[1] * n[2] - p[2] * n[1]  9.92 us
    dynamic_slice x8, local copies, waits for them, and re-layouts, round_terms(): lax.dynamic_index_in_dim(tgt_index, k, 0, keepdims=False)  5.5 us
    mul x8, other arithmetic, round_terms(): weight * resid  5.32 us
    mul x8, other arithmetic, round_terms(): blocks[:, :, :, None] * BLOCK  5.25 us
  transfers between devices with their start and end apart: 17, of which 3 were waited for; matrix products, arithmetic and copies ran while one was open for 79% of the time, Pallas kernels for 0%

commit v1 on v0

v1 whole, which is shorter than its diff:
```python
import functools

import jax
import jax.numpy as jnp
from jax import lax
from jax.experimental import pallas as pl
from jax.experimental.pallas import tpu as pltpu
from jax.sharding import PartitionSpec as P

BLOCK = 128
MESH = pl.DeviceIdType.MESH


def kernel(
    n, reps, pts, nrm, src, tgt, act, diag_ref, grad_ref, pair_ref,
    stage, inbox, prod, res, got, own, other,
    out_send, out_recv, back_send, back_recv, pair_send, pair_recv,
):
    rounds, per_rep = tgt.shape[0], tgt.shape[3]
    npts = pts.shape[1] * BLOCK
    me = lax.axis_index("blk")
    half = lax.axis_index("rep")
    partner = 1 - half

    offsets = sorted({k % n for k in range(1, rounds + 1)} | {-k % n for k in range(1, rounds + 1)})
    barrier = pltpu.get_barrier_semaphore()
    for d in offsets:
        for r in range(reps):
            pl.semaphore_signal(
                barrier, inc=1, device_id={"blk": lax.rem(me + d, n), "rep": r}, device_id_type=MESH
            )
    pl.semaphore_signal(barrier, inc=1, device_id={"blk": me, "rep": partner}, device_id_type=MESH)

    slot = lax.broadcasted_iota(jnp.int32, (per_rep, BLOCK), 0) + half * per_rep
    for k in range(rounds):
        for j in range(per_rep):
            block = src[k, 0, 0, j]
            for c in range(3):
                stage[k, c * per_rep + j, :] = pts[c, block]
        index = jnp.where(slot < act[0, k], tgt[k, 0, 0], npts)
        stage[k, 3 * per_rep :, :] = index.astype(jnp.float32)
    prod[...] = jnp.zeros_like(prod)
    res[...] = jnp.zeros_like(res)

    pl.semaphore_wait(barrier, len(offsets) * reps + 1)

    def outgoing(k):
        return pltpu.make_async_remote_copy(
            src_ref=stage.at[k],
            dst_ref=inbox.at[k],
            send_sem=out_send.at[k],
            recv_sem=out_recv.at[k],
            device_id={"blk": lax.rem(me + n - (k + 1), n), "rep": half},
            device_id_type=MESH,
        )

    def returned(k, r):
        return pltpu.make_async_remote_copy(
            src_ref=res.at[k],
            dst_ref=got.at[k, half],
            send_sem=back_send.at[k, r],
            recv_sem=back_recv.at[k, half],
            device_id={"blk": lax.rem(me + k + 1, n), "rep": r},
            device_id_type=MESH,
        )

    def arrival(k, r):
        return pltpu.make_async_remote_copy(
            src_ref=res.at[k],
            dst_ref=got.at[k, r],
            send_sem=back_send.at[k, r],
            recv_sem=back_recv.at[k, r],
            device_id={"blk": lax.rem(me + k + 1, n), "rep": r},
            device_id_type=MESH,
        )

    for k in range(rounds):
        outgoing(k).start()

    def one_round(k, carry):
        outgoing(k).wait_recv()
        p = [inbox[k, c * per_rep : (c + 1) * per_rep, :] for c in range(3)]
        index = inbox[k, 3 * per_rep :, :].astype(jnp.int32)
        lane = index & (BLOCK - 1)
        row = index >> (BLOCK.bit_length() - 1)
        found = [jnp.zeros((per_rep, BLOCK), jnp.float32) for _ in range(6)]
        for h in range(npts // BLOCK):
            here = row == h
            for c in range(6):
                table = pts if c < 3 else nrm
                line = table[c % 3, h : h + 1, :]
                line = jnp.broadcast_to(line, (per_rep, BLOCK))
                value = jnp.take_along_axis(line, lane, axis=1, mode="promise_in_bounds")
                found[c] = jnp.where(here, value, found[c])
        q, m = found[:3], found[3:]
        resid = m[0] * (p[0] - q[0]) + m[1] * (p[1] - q[1]) + m[2] * (p[2] - q[2])
        weight = 1.0 / (1.0 + resid * resid)
        jacob = [
            p[1] * m[2] - p[2] * m[1],
            p[2] * m[0] - p[0] * m[2],
            p[0] * m[1] - p[1] * m[0],
            m[0],
            m[1],
            m[2],
        ]
        for i in range(6):
            scaled = jacob[i] * weight
            for j in range(i, 6):
                line = jnp.sum(scaled * jacob[j], axis=0, keepdims=True)
                prod[k, 6 * i + j : 6 * i + j + 1, :] = line
                if j != i:
                    prod[k, 6 * j + i : 6 * j + i + 1, :] = line
            prod[k, 36 + i : 37 + i, :] = jnp.sum(scaled * resid, axis=0, keepdims=True)
        return carry

    lax.fori_loop(0, rounds, one_round, 0)

    width = prod.shape[1]
    ones = jnp.ones((8, BLOCK), jnp.float32)
    for k in range(rounds):
        sums = lax.dot_general(
            ones, prod[k], (((1,), (1,)), ((), ())),
            precision=lax.Precision.HIGHEST, preferred_element_type=jnp.float32,
        )
        res[k, :, :width] = sums[:1] / (reps * per_rep * BLOCK)
    for k in range(rounds):
        for r in range(reps):
            returned(k, r).start()
    lanes = lax.broadcasted_iota(jnp.int32, (1, BLOCK), 1)
    sign = jnp.where(lanes < 36, 1.0, -1.0)
    total = res[0]
    for k in range(1, rounds):
        total = total + res[k]
    own[...] = total * sign
    swap = pltpu.make_async_remote_copy(
        src_ref=own,
        dst_ref=other,
        send_sem=pair_send,
        recv_sem=pair_recv,
        device_id={"blk": me, "rep": partner},
        device_id_type=MESH,
    )
    swap.start()
    for k in range(rounds):
        outgoing(k).wait_send()
    swap.wait()
    total = own[...] + other[...]
    for k in range(rounds):
        for r in range(reps):
            arrival(k, r).wait_recv()
        both = got[k, 0] + got[k, 1]
        pair_ref[k, 0] = both[:, :36]
        total = total + both
    scale = 2.0 * rounds
    total = total / scale
    diag_ref[...] = total[:, :36]
    grad_ref[...] = total[:, 36:42]
    for k in range(rounds):
        for r in range(reps):
            returned(k, r).wait_send()


def by_rows(scan):
    return jnp.moveaxis(scan, 1, 0).reshape(scan.shape[1], -1, BLOCK)


def body(n, reps, points, normals, src_block, tgt_index, active):
    rounds, count = src_block.shape[:2]
    per_rep = src_block.shape[3]
    if count != 1 or reps != 2 or rounds >= n:
        raise ValueError("unsupported sizes")
    vmem = pl.BlockSpec(memory_space=pltpu.VMEM)
    smem = pl.BlockSpec(memory_space=pltpu.SMEM)
    f32 = jnp.float32
    return pl.pallas_call(
        functools.partial(kernel, n, reps),
        out_shape=(
            jax.ShapeDtypeStruct((1, 36), f32),
            jax.ShapeDtypeStruct((1, 6), f32),
            jax.ShapeDtypeStruct((rounds, 1, 1, 36), f32),
        ),
        in_specs=[vmem, vmem, smem, vmem, smem],
        out_specs=(vmem, vmem, vmem),
        scratch_shapes=[
            pltpu.VMEM((rounds, 4 * per_rep, BLOCK), f32),
            pltpu.VMEM((rounds, 4 * per_rep, BLOCK), f32),
            pltpu.VMEM((rounds, 48, BLOCK), f32),
            pltpu.VMEM((rounds, 1, BLOCK), f32),
            pltpu.VMEM((rounds, reps, 1, BLOCK), f32),
            pltpu.VMEM((1, BLOCK), f32),
            pltpu.VMEM((1, BLOCK), f32),
            pltpu.SemaphoreType.DMA((rounds,)),
            pltpu.SemaphoreType.DMA((rounds,)),
            pltpu.SemaphoreType.DMA((rounds, reps)),
            pltpu.SemaphoreType.DMA((rounds, reps)),
            pltpu.SemaphoreType.DMA,
            pltpu.SemaphoreType.DMA,
        ],
        compiler_params=pltpu.CompilerParams(collective_id=0, has_side_effects=True),
        name="normal_equations",
    )(by_rows(points), by_rows(normals), src_block, tgt_index, active.reshape(1, rounds))


def solution(mesh):
    return jax.shard_map(
        functools.partial(body, mesh.shape["blk"], mesh.shape["rep"]),
        mesh=mesh,
        in_specs=(
            P("blk", None, None),
            P("blk", None, None),
            P(None, "blk", None, "rep"),
            P(None, "blk", None, "rep", None),
            P(None, "blk", None),
        ),
        out_specs=(P("blk", None), P("blk", None), P(None, "blk", None, None)),
        check_vma=False,
    )
```

time: 186 us -> 26 us (0.14)
  local copies, waits for them, and re-layouts: 122 us -> 2.29 us
  other arithmetic: 26.3 us -> 0 us
  starting transfers between devices: 25.7 us -> 0 us
  Pallas kernels: 0 us -> 22.9 us
  waiting for transfers between devices: 3.48 us -> 0 us
  blocking collectives: 3.04 us -> 0 us
  matrix products: 2.67 us -> 0 us
    gather x16 -> x0, local copies, waits for them, and re-layouts: 79.8 us -> none  [the longest x8 39.9 us: round_terms(): picked = flat_tgt[:, tidx]]
    ppermute x17 -> x0, starting transfers between devices: 25.7 us -> none  [passed_along(): return lax.ppermute(block, axis, route)]
    pallas_call x0 -> x1, Pallas kernels: none -> 22.9 us  [body(): pl.pallas_call(functools.partial(kernel, n, reps), out_shape=(jax.ShapeDt...]
    ppermute x8 -> x0, local copies, waits for them, and re-layouts: 21.6 us -> none  [passed_along(): return lax.ppermute(block, axis, route)]
    mul x24 -> x0, other arithmetic: 10.8 us -> none  [the longest x8 5.32 us: round_terms(): weight * resid]
    dynamic_slice x16 -> x0, local copies, waits for them, and re-layouts: 10.2 us -> none  [the longest x8 5.5 us: round_terms(): lax.dynamic_index_in_dim(tgt_index, k, 0, keepdims=False)]
    sub x8 -> x0, other arithmetic: 9.92 us -> none  [round_terms(): p[1] * n[2] - p[2] * n[1]]
    ppermute x17 -> x0, waiting for transfers between devices: 3.48 us -> none  [passed_along(): return lax.ppermute(block, axis, route)]
  transfers between devices with their start and end apart: 17 -> 0, of which waited for: 3 -> 0; matrix products, arithmetic and copies ran while one was open for 79% -> 0% of each run, Pallas kernels for 0% -> 0%
where the time goes in v1:
time: 26 us; the launch traced here: 25.8 us
  Pallas kernels  22.9 us (88%)
  local copies, waits for them, and re-layouts  2.29 us (9%)
  between operations  0.66 us (3%)
    pallas_call x1, Pallas kernels, body(): pl.pallas_call(functools.partial(kernel, n, reps), out_shape=(jax.ShapeDt...  22.9 us
    unnamed x9, local copies, waits for them, and re-layouts  2.29 us

profile of v1, /device:TPU:0, one launch (start us, length us, event | category | flops | bytes accessed | tf_op | source)
XLA Modules:
  0.0 25.8 jit_solution(8741141957216397459)
XLA Ops:
  0.6 22.9 %normal_equations.1 = (f32[1,36]{1,0:T(1,128)}, f32[1,6]{1,0:T(1,128)}, f32[8,1,1,36]{3,2,1,0:T(1,128)}) custom-call(f32[3,64,128]{2,1,0:T(8,128)} %bitcast.3, f32[3,64,128]{2,1,0:T(8,128)} %bitcast.4, s32[8,1,1,8]{3,2,1,0:T(1,128)} %src.1, s32[8,1,1,8,128]{4,3,2,1,0:T(8,128)} %tgt.1, s32[1,8]{1,0:T(1,128)} %bitcast.5), custom_call_target="tpu_custom_call" | custom-call | tf_op jit(solution)/shard_map/normal_equations/pallas_call | solution.py:175
  23.5 0.0 copy-start.2
  23.5 0.0 copy-start
  23.5 0.6 %copy-done.2 = f32[1,36]{1,0:T(1,128)S(1)} copy-done((f32[1,36]{1,0:T(1,128)S(1)}, f32[1,36]{1,0:T(1,128)}, u32[]{:S(2)}) %copy-start.2) | copy-done | bytes 168
  24.1 0.0 copy-start.1
  24.1 0.5 %copy.11 = f32[1,36]{1,0:T(1,128)} copy(f32[1,36]{1,0:T(1,128)S(1)} %copy-done.2) | data formatting | bytes 288
  24.7 0.1 copy-done.1
  24.7 0.5 %copy.12 = f32[1,6]{1,0:T(1,128)} copy(f32[1,6]{1,0:T(1,128)S(1)} %copy-done.1) | data formatting | bytes 48
  25.2 0.0 copy-done
  25.2 0.6 %copy.13 = f32[8,1,1,36]{3,2,1,0:T(1,128)} copy(f32[8,1,1,36]{3,2,1,0:T(1,128)S(1)} %copy-done) | data formatting | bytes 2304
Async XLA Ops:
  23.5 0.6 %copy-start.2 = (f32[1,36]{1,0:T(1,128)S(1)}, f32[1,36]{1,0:T(1,128)}, u32[]{:S(2)}) copy-start(f32[1,36]{1,0:T(1,128)} %get-tuple-element.6) | copy-start | bytes 436
  23.5 1.7 %copy-start = (f32[8,1,1,36]{3,2,1,0:T(1,128)S(1)}, f32[8,1,1,36]{3,2,1,0:T(1,128)}, u32[]{:S(2)}) copy-start(f32[8,1,1,36]{3,2,1,0:T(1,128)} %get-tuple-element.8) | copy-start | bytes 3460
  24.1 0.6 %copy-start.1 = (f32[1,6]{1,0:T(1,128)S(1)}, f32[1,6]{1,0:T(1,128)}, u32[]{:S(2)}) copy-start(f32[1,6]{1,0:T(1,128)} %get-tuple-element.7) | copy-start | bytes 76

commit v2 on v1

--- a/solution.py
+++ b/solution.py
@@ -11,16 +11,23 @@
 MESH = pl.DeviceIdType.MESH
 
 
+def schedule(rounds):
+    bits = sorted(range(1, rounds + 1), key=lambda k: (k.bit_count(), k))
+    near = [k for k in bits if k.bit_count() == 1]
+    return [k - 1 for k in near[1:2] + near[3:] + near[:1] + bits[len(near) :] + near[2:3]]
+
+
 def kernel(
-    n, reps, pts, nrm, src, tgt, act, diag_ref, grad_ref, pair_ref,
-    stage, inbox, prod, res, got, own, other,
-    out_send, out_recv, back_send, back_recv, pair_send, pair_recv,
+    n, reps, pts_hbm, nrm_hbm, src_hbm, tgt_hbm, act_hbm, out,
+    pts, nrm, src, tgt, act, stage, inbox, prod, res, got, own, other,
+    load, out_send, out_recv, back_send, back_recv, pair_send, pair_recv,
 ):
     rounds, per_rep = tgt.shape[0], tgt.shape[3]
     npts = pts.shape[1] * BLOCK
     me = lax.axis_index("blk")
     half = lax.axis_index("rep")
     partner = 1 - half
+    order = schedule(rounds)
 
     offsets = sorted({k % n for k in range(1, rounds + 1)} | {-k % n for k in range(1, rounds + 1)})
     barrier = pltpu.get_barrier_semaphore()
@@ -31,6 +38,15 @@
             )
     pl.semaphore_signal(barrier, inc=1, device_id={"blk": me, "rep": partner}, device_id_type=MESH)
 
+    pairs = ((src_hbm, src), (act_hbm, act), (tgt_hbm, tgt), (pts_hbm, pts), (nrm_hbm, nrm))
+    loads = [pltpu.make_async_copy(a, b, load.at[i]) for i, (a, b) in enumerate(pairs)]
+    for copy in loads:
+        copy.start()
+    prod[...] = jnp.zeros_like(prod)
+    res[...] = jnp.zeros_like(res)
+    for copy in loads[:4]:
+        copy.wait()
+
     slot = lax.broadcasted_iota(jnp.int32, (per_rep, BLOCK), 0) + half * per_rep
     for k in range(rounds):
         for j in range(per_rep):
@@ -39,8 +55,6 @@
                 stage[k, c * per_rep + j, :] = pts[c, block]
         index = jnp.where(slot < act[0, k], tgt[k, 0, 0], npts)
         stage[k, 3 * per_rep :, :] = index.astype(jnp.float32)
-    prod[...] = jnp.zeros_like(prod)
-    res[...] = jnp.zeros_like(res)
 
     pl.semaphore_wait(barrier, len(offsets) * reps + 1)
 
@@ -74,11 +88,11 @@
             device_id_type=MESH,
         )
 
-    for k in range(rounds):
+    for k in order:
         outgoing(k).start()
-
-    def one_round(k, carry):
-        outgoing(k).wait_recv()
+    loads[4].wait()
+
+    def terms(k):
         p = [inbox[k, c * per_rep : (c + 1) * per_rep, :] for c in range(3)]
         index = inbox[k, 3 * per_rep :, :].astype(jnp.int32)
         lane = index & (BLOCK - 1)
@@ -111,21 +125,30 @@
                 if j != i:
                     prod[k, 6 * j + i : 6 * j + i + 1, :] = line
             prod[k, 36 + i : 37 + i, :] = jnp.sum(scaled * resid, axis=0, keepdims=True)
-        return carry
-
-    lax.fori_loop(0, rounds, one_round, 0)
 
     width = prod.shape[1]
     ones = jnp.ones((8, BLOCK), jnp.float32)
-    for k in range(rounds):
+
+    def lane_sums(k):
         sums = lax.dot_general(
             ones, prod[k], (((1,), (1,)), ((), ())),
             precision=lax.Precision.HIGHEST, preferred_element_type=jnp.float32,
         )
         res[k, :, :width] = sums[:1] / (reps * per_rep * BLOCK)
-    for k in range(rounds):
-        for r in range(reps):
-            returned(k, r).start()
+
+    before = None
+    for k in order:
+        outgoing(k).wait_recv()
+        if before is not None:
+            lane_sums(before)
+        terms(k)
+        if before is not None:
+            for r in range(reps):
+                returned(before, r).start()
+        before = k
+    lane_sums(before)
+    for r in range(reps):
+        returned(before, r).start()
     lanes = lax.broadcasted_iota(jnp.int32, (1, BLOCK), 1)
     sign = jnp.where(lanes < 36, 1.0, -1.0)
     total = res[0]
@@ -141,23 +164,28 @@
         device_id_type=MESH,
     )
     swap.start()
-    for k in range(rounds):
+    for k in order:
         outgoing(k).wait_send()
     swap.wait()
     total = own[...] + other[...]
-    for k in range(rounds):
+    for k in order:
         for r in range(reps):
             arrival(k, r).wait_recv()
         both = got[k, 0] + got[k, 1]
-        pair_ref[k, 0] = both[:, :36]
+        out[k : k + 1, :] = both
         total = total + both
-    scale = 2.0 * rounds
-    total = total / scale
-    diag_ref[...] = total[:, :36]
-    grad_ref[...] = total[:, 36:42]
-    for k in range(rounds):
+    out[rounds : rounds + 1, :] = total / (2.0 * rounds)
+    for k in order:
         for r in range(reps):
             returned(k, r).wait_send()
+
+
+def split(sums, diag_ref, grad_ref, pair_ref):
+    rounds = pair_ref.shape[0]
+    for k in range(rounds):
+        pair_ref[k, 0] = sums[k : k + 1, :36]
+    diag_ref[...] = sums[rounds : rounds + 1, :36]
+    grad_ref[...] = sums[rounds : rounds + 1, 36:42]
 
 
 def by_rows(scan):
@@ -170,18 +198,19 @@
     if count != 1 or reps != 2 or rounds >= n:
         raise ValueError("unsupported sizes")
     vmem = pl.BlockSpec(memory_space=pltpu.VMEM)
-    smem = pl.BlockSpec(memory_space=pltpu.SMEM)
-    f32 = jnp.float32
-    return pl.pallas_call(
+    f32, i32 = jnp.float32, jnp.int32
+    rows = points.shape[2] // BLOCK
+    sums = pl.pallas_call(
         functools.partial(kernel, n, reps),
-        out_shape=(
-            jax.ShapeDtypeStruct((1, 36), f32),
-            jax.ShapeDtypeStruct((1, 6), f32),
-            jax.ShapeDtypeStruct((rounds, 1, 1, 36), f32),
-        ),
-        in_specs=[vmem, vmem, smem, vmem, smem],
-        out_specs=(vmem, vmem, vmem),
+        out_shape=jax.ShapeDtypeStruct((rounds + 1, BLOCK), f32),
+        in_specs=[pl.BlockSpec(memory_space=pl.ANY)] * 5,
+        out_specs=vmem,
         scratch_shapes=[
+            pltpu.VMEM((3, rows, BLOCK), f32),
+            pltpu.VMEM((3, rows, BLOCK), f32),
+            pltpu.SMEM(src_block.shape, i32),
+            pltpu.VMEM(tgt_index.shape, i32),
+            pltpu.SMEM((1, rounds), i32),
             pltpu.VMEM((rounds, 4 * per_rep, BLOCK), f32),
             pltpu.VMEM((rounds, 4 * per_rep, BLOCK), f32),
             pltpu.VMEM((rounds, 48, BLOCK), f32),
@@ -189,6 +218,7 @@
             pltpu.VMEM((rounds, reps, 1, BLOCK), f32),
             pltpu.VMEM((1, BLOCK), f32),
             pltpu.VMEM((1, BLOCK), f32),
+            pltpu.SemaphoreType.DMA((5,)),
             pltpu.SemaphoreType.DMA((rounds,)),
             pltpu.SemaphoreType.DMA((rounds,)),
             pltpu.SemaphoreType.DMA((rounds, reps)),
@@ -199,6 +229,17 @@
         compiler_params=pltpu.CompilerParams(collective_id=0, has_side_effects=True),
         name="normal_equations",
     )(by_rows(points), by_rows(normals), src_block, tgt_index, active.reshape(1, rounds))
+    return pl.pallas_call(
+        split,
+        out_shape=(
+            jax.ShapeDtypeStruct((1, 36), f32),
+            jax.ShapeDtypeStruct((1, 6), f32),
+            jax.ShapeDtypeStruct((rounds, 1, 1, 36), f32),
+        ),
+        in_specs=[vmem],
+        out_specs=(vmem, vmem, vmem),
+        name="split_sums",
+    )(sums)
 
 
 def solution(mesh):

time: 26 us -> 21.3 us (0.82)
  Pallas kernels: 22.9 us -> 20.4 us
  local copies, waits for them, and re-layouts: 2.29 us -> 0 us
    pallas_call x1 -> x2, Pallas kernels: 22.9 us -> 20.4 us  [the longest x1 19 us: body(): pl.pallas_call(functools.partial(kernel, n, reps), out_shape=jax.ShapeDty...]
    unnamed x9 -> x0, local copies, waits for them, and re-layouts: 2.29 us -> none
where the time goes in v2:
time: 21.3 us; the launch traced here: 21 us
  Pallas kernels  20.4 us (96%)
  between operations  0.64 us (3%)
    pallas_call x1, Pallas kernels, body(): pl.pallas_call(functools.partial(kernel, n, reps), out_shape=jax.ShapeDty...  19 us
    pallas_call x1, Pallas kernels, body(): pl.pallas_call(split, out_shape=(jax.ShapeDtypeStruct((1, 36), f32), jax....  1.36 us

profile of v2, /device:TPU:0, one launch (start us, length us, event | category | flops | bytes accessed | tf_op | source)
XLA Modules:
  0.0 21.0 jit_solution(4347500192522642687)
XLA Ops:
  0.6 19.0 %normal_equations.1.sums = f32[9,128]{1,0:T(8,128)} custom-call(f32[3,64,128]{2,1,0:T(8,128)} %bitcast.3, f32[3,64,128]{2,1,0:T(8,128)} %bitcast.4, s32[8,1,1,8]{3,2,1,0:T(1,128)} %src_hbm.1, s32[8,1,1,8,128]{4,3,2,1,0:T(8,128)} %tgt_hbm.1, s32[1,8]{1,0:T(1,128)} %bitcast.5), custom_call_target="tpu_custom_call" | custom-call | tf_op jit(solution)/shard_map/normal_equations/pallas_call | solution.py:203
  19.7 1.4 %split_sums.1 = (f32[1,36]{1,0:T(1,128)}, f32[1,6]{1,0:T(1,128)}, f32[8,1,1,36]{3,2,1,0:T(1,128)}) custom-call(f32[9,128]{1,0:T(8,128)} %normal_equations.1.sums), custom_call_target="tpu_custom_call" | custom-call | tf_op jit(solution)/shard_map/split_sums/pallas_call | solution.py:232

commit v3 on v2

--- a/solution.py
+++ b/solution.py
@@ -202,7 +202,7 @@
     rows = points.shape[2] // BLOCK
     sums = pl.pallas_call(
         functools.partial(kernel, n, reps),
-        out_shape=jax.ShapeDtypeStruct((rounds + 1, BLOCK), f32),
+        out_shape=pltpu.VMEM((rounds + 1, BLOCK), f32),
         in_specs=[pl.BlockSpec(memory_space=pl.ANY)] * 5,
         out_specs=vmem,
         scratch_shapes=[
@@ -239,7 +239,7 @@
         in_specs=[vmem],
         out_specs=(vmem, vmem, vmem),
         name="split_sums",
-    )(sums)
+    )(pltpu.with_memory_space_constraint(sums, pltpu.VMEM))
 
 
 def solution(mesh):

time: 21.3 us -> 19.9 us (0.934)
  Pallas kernels: 20.4 us -> 19.1 us
    pallas_call x1, Pallas kernels: 1.36 us -> 0.67 us  [body(): pl.pallas_call(split, out_shape=(jax.ShapeDtypeStruct((1, 36), f32), jax....]
    pallas_call x1, Pallas kernels: 19 us -> 18.4 us  [body(): pl.pallas_call(functools.partial(kernel, n, reps), out_shape=pltpu.VMEM((...]
where the time goes in v3:
time: 19.9 us; the launch traced here: 19.7 us
  Pallas kernels  19.1 us (96%)
  between operations  0.64 us (3%)
    pallas_call x1, Pallas kernels, body(): pl.pallas_call(functools.partial(kernel, n, reps), out_shape=pltpu.VMEM((...  18.4 us
    pallas_call x1, Pallas kernels, body(): pl.pallas_call(split, out_shape=(jax.ShapeDtypeStruct((1, 36), f32), jax....  0.67 us

profile of v3, /device:TPU:0, one launch (start us, length us, event | category | flops | bytes accessed | tf_op | source)
XLA Modules:
  0.0 19.7 jit_solution(10941889474137339518)
XLA Ops:
  0.6 18.4 %normal_equations.1.sums = f32[9,128]{1,0:T(8,128)S(1)} custom-call(f32[3,64,128]{2,1,0:T(8,128)} %bitcast.3, f32[3,64,128]{2,1,0:T(8,128)} %bitcast.4, s32[8,1,1,8]{3,2,1,0:T(1,128)} %src_hbm.1, s32[8,1,1,8,128]{4,3,2,1,0:T(8,128)} %tgt_hbm.1, s32[1,8]{1,0:T(1,128)} %bitcast.5), custom_call_target="tpu_custom_call" | custom-call | tf_op jit(solution)/shard_map/normal_equations/pallas_call | solution.py:203
  19.1 0.7 %split_sums.1 = (f32[1,36]{1,0:T(1,128)}, f32[1,6]{1,0:T(1,128)}, f32[8,1,1,36]{3,2,1,0:T(1,128)}) custom-call(f32[9,128]{1,0:T(8,128)S(1)} %normal_equations.1.sums), custom_call_target="tpu_custom_call" | custom-call | tf_op jit(solution)/shard_map/split_sums/pallas_call | solution.py:232

commit v4 on v3

--- a/solution.py
+++ b/solution.py
@@ -32,10 +32,9 @@
     offsets = sorted({k % n for k in range(1, rounds + 1)} | {-k % n for k in range(1, rounds + 1)})
     barrier = pltpu.get_barrier_semaphore()
     for d in offsets:
-        for r in range(reps):
-            pl.semaphore_signal(
-                barrier, inc=1, device_id={"blk": lax.rem(me + d, n), "rep": r}, device_id_type=MESH
-            )
+        pl.semaphore_signal(
+            barrier, inc=1, device_id={"blk": lax.rem(me + d, n), "rep": half}, device_id_type=MESH
+        )
     pl.semaphore_signal(barrier, inc=1, device_id={"blk": me, "rep": partner}, device_id_type=MESH)
 
     pairs = ((src_hbm, src), (act_hbm, act), (tgt_hbm, tgt), (pts_hbm, pts), (nrm_hbm, nrm))
@@ -56,7 +55,7 @@
         index = jnp.where(slot < act[0, k], tgt[k, 0, 0], npts)
         stage[k, 3 * per_rep :, :] = index.astype(jnp.float32)
 
-    pl.semaphore_wait(barrier, len(offsets) * reps + 1)
+    pl.semaphore_wait(barrier, len(offsets) + 1)
 
     def outgoing(k):
         return pltpu.make_async_remote_copy(
@@ -68,23 +67,13 @@
             device_id_type=MESH,
         )
 
-    def returned(k, r):
+    def returned(k):
         return pltpu.make_async_remote_copy(
             src_ref=res.at[k],
-            dst_ref=got.at[k, half],
-            send_sem=back_send.at[k, r],
-            recv_sem=back_recv.at[k, half],
-            device_id={"blk": lax.rem(me + k + 1, n), "rep": r},
-            device_id_type=MESH,
-        )
-
-    def arrival(k, r):
-        return pltpu.make_async_remote_copy(
-            src_ref=res.at[k],
-            dst_ref=got.at[k, r],
-            send_sem=back_send.at[k, r],
-            recv_sem=back_recv.at[k, r],
-            device_id={"blk": lax.rem(me + k + 1, n), "rep": r},
+            dst_ref=got.at[k],
+            send_sem=back_send.at[k],
+            recv_sem=back_recv.at[k],
+            device_id={"blk": lax.rem(me + k + 1, n), "rep": half},
             device_id_type=MESH,
         )
 
@@ -143,18 +132,23 @@
             lane_sums(before)
         terms(k)
         if before is not None:
-            for r in range(reps):
-                returned(before, r).start()
+            returned(before).start()
         before = k
     lane_sums(before)
-    for r in range(reps):
-        returned(before, r).start()
+    returned(before).start()
     lanes = lax.broadcasted_iota(jnp.int32, (1, BLOCK), 1)
     sign = jnp.where(lanes < 36, 1.0, -1.0)
     total = res[0]
     for k in range(1, rounds):
         total = total + res[k]
-    own[...] = total * sign
+    total = total * sign
+    for k in order:
+        outgoing(k).wait_send()
+    for k in order:
+        returned(k).wait_recv()
+        own[k : k + 1, :] = got[k]
+        total = total + got[k]
+    own[rounds : rounds + 1, :] = total / (2.0 * rounds)
     swap = pltpu.make_async_remote_copy(
         src_ref=own,
         dst_ref=other,
@@ -165,19 +159,9 @@
     )
     swap.start()
     for k in order:
-        outgoing(k).wait_send()
+        returned(k).wait_send()
     swap.wait()
-    total = own[...] + other[...]
-    for k in order:
-        for r in range(reps):
-            arrival(k, r).wait_recv()
-        both = got[k, 0] + got[k, 1]
-        out[k : k + 1, :] = both
-        total = total + both
-    out[rounds : rounds + 1, :] = total / (2.0 * rounds)
-    for k in order:
-        for r in range(reps):
-            returned(k, r).wait_send()
+    out[...] = own[...] + other[...]
 
 
 def split(sums, diag_ref, grad_ref, pair_ref):
@@ -215,14 +199,14 @@
             pltpu.VMEM((rounds, 4 * per_rep, BLOCK), f32),
             pltpu.VMEM((rounds, 48, BLOCK), f32),
             pltpu.VMEM((rounds, 1, BLOCK), f32),
-            pltpu.VMEM((rounds, reps, 1, BLOCK), f32),
-            pltpu.VMEM((1, BLOCK), f32),
-            pltpu.VMEM((1, BLOCK), f32),
+            pltpu.VMEM((rounds, 1, BLOCK), f32),
+            pltpu.VMEM((rounds + 1, BLOCK), f32),
+            pltpu.VMEM((rounds + 1, BLOCK), f32),
             pltpu.SemaphoreType.DMA((5,)),
             pltpu.SemaphoreType.DMA((rounds,)),
             pltpu.SemaphoreType.DMA((rounds,)),
-            pltpu.SemaphoreType.DMA((rounds, reps)),
-            pltpu.SemaphoreType.DMA((rounds, reps)),
+            pltpu.SemaphoreType.DMA((rounds,)),
+            pltpu.SemaphoreType.DMA((rounds,)),
             pltpu.SemaphoreType.DMA,
             pltpu.SemaphoreType.DMA,
         ],

time: 19.9 us -> 22.3 us (1.12)
  Pallas kernels: 19.1 us -> 21.5 us
    pallas_call x1, Pallas kernels: 18.4 us -> 20.8 us  [body(): pl.pallas_call(functools.partial(kernel, n, reps), out_shape=pltpu.VMEM((...]
where the time goes in v4:
time: 22.3 us; the launch traced here: 22.1 us
  Pallas kernels  21.5 us (96%)
  between operations  0.64 us (3%)
    pallas_call x1, Pallas kernels, body(): pl.pallas_call(functools.partial(kernel, n, reps), out_shape=pltpu.VMEM((...  20.8 us
    pallas_call x1, Pallas kernels, body(): pl.pallas_call(split, out_shape=(jax.ShapeDtypeStruct((1, 36), f32), jax....  0.67 us

profile of v4, /device:TPU:0, one launch (start us, length us, event | category | flops | bytes accessed | tf_op | source)
XLA Modules:
  0.0 22.1 jit_solution(146921500893549836)
XLA Ops:
  0.6 20.8 %normal_equations.1.sums = f32[9,128]{1,0:T(8,128)S(1)} custom-call(f32[3,64,128]{2,1,0:T(8,128)} %bitcast.3, f32[3,64,128]{2,1,0:T(8,128)} %bitcast.4, s32[8,1,1,8]{3,2,1,0:T(1,128)} %src_hbm.1, s32[8,1,1,8,128]{4,3,2,1,0:T(8,128)} %tgt_hbm.1, s32[1,8]{1,0:T(1,128)} %bitcast.5), custom_call_target="tpu_custom_call" | custom-call | tf_op jit(solution)/shard_map/normal_equations/pallas_call | solution.py:187
  21.4 0.7 %split_sums.1 = (f32[1,36]{1,0:T(1,128)}, f32[1,6]{1,0:T(1,128)}, f32[8,1,1,36]{3,2,1,0:T(1,128)}) custom-call(f32[9,128]{1,0:T(8,128)S(1)} %normal_equations.1.sums), custom_call_target="tpu_custom_call" | custom-call | tf_op jit(solution)/shard_map/split_sums/pallas_call | solution.py:216
